TPU v7x, 32 devices: a whole 2x2x4 slice. The times are simulated.
32 devices in a mesh: grp: 2 (over y), lay: 4 (over z), wid: 2 (over x), rep: 2 (over core).
Axes of the slice: x: 2, y: 2, z: 4, core: 2. Of those that a mesh axis runs over, the one named last changes fastest.
Arguments:
- acts: bfloat16 [4, 1024, 2048], P(None, ('grp', 'rep'), 'wid'), parts along dimension 1, may hold values from -6 to 6
- targets: bfloat16 [4, 1024, 2048], P(None, ('grp', 'rep'), 'wid'), parts along dimension 1, may hold values from -6 to 6
- enc_weight: bfloat16 [2048, 8192], P('wid', 'lay'), may hold values from -0.125 to 0.125
- enc_bias: float32 [8192], P('lay'), may hold values from -3 to 3
- gate_mask: int32 [1024, 32], P(('grp', 'rep'), 'lay'), parts along dimension 0, may hold values 0 or 1
- dec_list: int32 [84, 3], P('lay'), may hold values from -1 to 7, as said below
- dec_weight: bfloat16 [84, 256, 2048], P('lay', None, 'wid'), may hold values from -0.125 to 0.125
Outputs:
- grad_enc: float32 [4096, 8192], P(('grp', 'wid'), ('lay', 'rep')), parts along dimension 0
- grad_bias: float32 [16384], P(('grp', 'lay', 'rep')), parts along dimension 0
- grad_dec: float32 [168, 256, 2048], P(('grp', 'lay'), 'rep', 'wid'), parts along dimension 0
There are 2 independent parts, one for each index of `grp`. A program takes and returns all parts, laid end to end along the dimension named above; an argument that names none is the same for every part. Nothing has to cross between parts.
Inputs may be any that keep to these rules, and one draw needn't show every extreme that they name: `dec_list`: each row is (source layer, target layer, latent block within the layer's slab); every triple with source <= target < 4 and block < 8 stands in exactly one row; every other row is (-1, -1, -1).
All inputs are finite; a program needn't handle non-finite values. No bound on the sum of `gate_mask` on one device may be relied on, other than what follows from the above.
Results may differ from a plain program's by a relative error of at most 0.019.
Values may be sent and summed in bfloat16 or wider, within the bound.
A program may use at most 128 MiB of HBM per device.

v0:
```python
import jax
import jax.numpy as jnp
from jax import lax
from jax.sharding import PartitionSpec as P

ROOT = 0.7978845608028654
CUBIC = 0.044715


def smooth_gate(shifted):
    inside_arg = ROOT * (shifted + CUBIC * shifted * shifted * shifted)
    return 0.5 * shifted * (1.0 + jnp.tanh(inside_arg))


def gate_slope(shifted):
    inside_arg = ROOT * (shifted + CUBIC * shifted * shifted * shifted)
    tanh_part = jnp.tanh(inside_arg)
    return 0.5 * (1.0 + tanh_part) + 0.5 * shifted * (1.0 - tanh_part * tanh_part) * ROOT * (
        1.0 + 3.0 * CUBIC * shifted * shifted
    )


def local(acts, targets, enc_weight, enc_bias, gate_mask, dec_list, dec_weight):
    layers, tok_rows, width_part = acts.shape
    lat_dev = enc_weight.shape[1]
    block_size = dec_weight.shape[1]
    per_dev = lat_dev // block_size
    lay_count = lax.axis_size("lay")
    lay_index = lax.axis_index("lay")
    lat_total = lat_dev * lay_count
    blocks_total = lat_total // block_size
    latents_layer = lat_total // layers
    blocks_layer = latents_layer // block_size
    layer_here = lay_index * lat_dev // latents_layer
    inputs = lax.dynamic_index_in_dim(acts, layer_here, 0, keepdims=False)
    partial_pre = jnp.dot(inputs, enc_weight, preferred_element_type=jnp.float32)
    pre_sum = lax.psum(partial_pre.astype(jnp.bfloat16), "wid").astype(jnp.float32)
    shifted = (pre_sum + enc_bias[None, :]).reshape(tok_rows, per_dev, block_size)
    keep_mask = gate_mask.astype(jnp.float32)[:, :, None]
    latent = (smooth_gate(shifted) * keep_mask).astype(jnp.bfloat16).reshape(tok_rows, lat_dev)
    all_latent = lax.all_gather(latent, "lay", axis=1, tiled=True).reshape(
        tok_rows, blocks_total, block_size
    )
    block_id = dec_list[:, 0] * blocks_layer + dec_list[:, 2]
    target_layer = dec_list[:, 1]
    slot_valid = (target_layer >= 0).astype(jnp.float32)
    target_hot = (target_layer[:, None] == jnp.arange(layers, dtype=jnp.int32)[None, :]).astype(
        jnp.float32
    )
    block_hot = (block_id[:, None] == jnp.arange(blocks_total, dtype=jnp.int32)[None, :]).astype(
        jnp.float32
    )
    slot_lat = jnp.take(all_latent, jnp.maximum(block_id, 0), axis=1)
    contrib = jnp.einsum("tkb,kbd->ktd", slot_lat, dec_weight, preferred_element_type=jnp.float32)
    recon_part = jnp.einsum("kl,ktd->ltd", target_hot, contrib, precision=lax.Precision.HIGHEST)
    recon = lax.psum_scatter(
        recon_part.astype(jnp.bfloat16), "lay", scatter_dimension=1, tiled=True
    ).astype(jnp.float32)
    row_count = recon.shape[1]
    own_target = lax.dynamic_slice_in_dim(targets, lay_index * row_count, row_count, 1)
    scale = float(tok_rows * lax.axis_size("rep")) ** (-0.5)
    scaled_error = ((recon - own_target.astype(jnp.float32)) * scale).astype(jnp.bfloat16)
    error_full = lax.all_gather(scaled_error, "lay", axis=1, tiled=True)
    err_slot = jnp.take(error_full, jnp.maximum(target_layer, 0), axis=0)
    dec_grad = (
        jnp.einsum("tkb,ktd->kbd", slot_lat, err_slot, preferred_element_type=jnp.float32)
        * slot_valid[:, None, None]
    )
    slot_error = jnp.einsum(
        "ktd,kbd->tkb", err_slot, dec_weight, preferred_element_type=jnp.float32
    )
    summed = lax.psum(slot_error.astype(jnp.bfloat16), "wid").astype(jnp.float32)
    outgoing = jnp.einsum("tkb,kg->tgb", summed, block_hot, precision=lax.Precision.HIGHEST).astype(
        jnp.bfloat16
    )
    incoming = lax.all_to_all(outgoing, "lay", split_axis=1, concat_axis=1, tiled=True)
    latent_error = jnp.sum(
        incoming.reshape(tok_rows, lay_count, per_dev, block_size), axis=1, dtype=jnp.float32
    )
    pre_grad = (latent_error * keep_mask * gate_slope(shifted)).astype(jnp.bfloat16)
    pre_flat = pre_grad.reshape(tok_rows, lat_dev)
    enc_grad = lax.dot_general(
        inputs, pre_flat, (((0,), (0,)), ((), ())), preferred_element_type=jnp.float32
    )
    bias_grad = jnp.sum(pre_flat, axis=0, dtype=jnp.float32)
    enc_out, bias_out, dec_out = (
        lax.psum_scatter(
            enc_grad.astype(jnp.bfloat16), "rep", scatter_dimension=1, tiled=True
        ).astype(jnp.float32),
        lax.psum_scatter(
            bias_grad.astype(jnp.bfloat16), "rep", scatter_dimension=0, tiled=True
        ).astype(jnp.float32),
        lax.psum_scatter(
            dec_grad.astype(jnp.bfloat16), "rep", scatter_dimension=1, tiled=True
        ).astype(jnp.float32),
    )
    return (enc_out, bias_out, dec_out)


def solution(mesh):
    return jax.shard_map(
        local,
        mesh=mesh,
        in_specs=(
            P(None, ("grp", "rep"), "wid"),
            P(None, ("grp", "rep"), "wid"),
            P("wid", "lay"),
            P("lay"),
            P(("grp", "rep"), "lay"),
            P("lay", None),
            P("lay", None, "wid"),
        ),
        out_specs=(
            P(("grp", "wid"), ("lay", "rep")),
            P(("grp", "lay", "rep")),
            P(("grp", "lay"), "rep", "wid"),
        ),
        check_vma=False,
    )
```

profile of v0, /device:TPU:15, one launch (start us, length us, event | category | flops | bytes accessed | tf_op | source)
XLA Modules:
  0.0 585.1 jit_solution(1712257840101359199)
XLA Ops:
  8.8 4.4 convolution_convert_fusion.1
  16.0 37.4 %all-reduce.6.cloned.1.call-done = bf16[256,2048]{1,0:T(8,128)(2,1)} async-done(((bf16[256,2048]{1,0:T(8,128)(2,1)}), bf16[256,2048]{1,0:T(8,128)(2,1)}) %all-reduce.6.cloned.1.call-update) | async-done | bytes 1048592 | tf_op jit(solution)/shard_map/psum | solution.py:37
  53.5 3.7 multiply_convert_fusion.1
  57.3 79.2 %all-gather.3.cloned.1.call-done = bf16[256,8192]{1,0:T(8,128)(2,1)} async-done(((bf16[256,2048]{1,0:T(8,128)(2,1)}), bf16[256,8192]{1,0:T(8,128)(2,1)}) %all-gather.3.cloned.1.call-update) | async-done | bytes 4194320 | tf_op jit(solution)/shard_map/all_gather | solution.py:41
  136.5 4.7 copy.50
  141.2 4.6 gather_fusion
  145.8 15.3 %fusion.6 = f32[21,256,1024]{2,1,0:T(8,128)} fusion(bf16[21,256,1024]{2,1,0:T(8,128)(2,1)} %param.13, bf16[21,256,256]{2,1,0:T(8,128)(2,1)} %gather_fusion, pred[21]{0:T(512)(128)(4,1)S(1)} %get-tuple-element.5), kind=kOutput, calls=%fused_computation.16 | convolution fusion | flops 2819948544 | bytes 35782676 | tf_op jit(solution)/shard_map/tkb,kbd->ktd/dot_general | solution.py:54
  161.1 28.4 %fusion.19 = bf16[4,256,1024]{2,0,1:T(4,128)(2,1)} fusion(f32[21,256,1024]{2,1,0:T(8,128)} %fusion.6, s32[21]{0:T(128)S(1)} %get-tuple-element.9), kind=kOutput, calls=%fused_computation.32 | convolution fusion | flops 265289808 | bytes 24117332 | tf_op jit(solution)/shard_map/kl,ktd->ltd/dot_general | solution.py:55
  192.0 83.4 %all-reduce.10.cloned.1.call-done = bf16[4,256,1024]{2,0,1:T(4,128)(2,1)} async-done(((bf16[4,256,1024]{2,0,1:T(4,128)(2,1)}), bf16[4,256,1024]{2,0,1:T(4,128)(2,1)}) %all-reduce.10.cloned.1.call-update) | async-done | bytes 2097168
  275.4 2.5 multiply_convert_fusion.2
  277.9 44.6 %all-gather.5.cloned.1.call-done = bf16[4,256,1024]{2,0,1:T(4,128)(2,1)} async-done(((bf16[4,64,1024]{2,0,1:T(4,128)(2,1)}), bf16[4,256,1024]{2,0,1:T(4,128)(2,1)}) %all-gather.5.cloned.1.call-update) | async-done | bytes 2097168 | tf_op jit(solution)/shard_map/all_gather | solution.py:63
  322.5 3.5 copy.30
  326.0 7.4 %gather_fusion.1 = bf16[21,256,1024]{2,1,0:T(8,128)(2,1)} fusion(bf16[4,256,1024]{2,1,0:T(8,128)(2,1)} %copy.30, s32[1024]{0:T(1024)S(1)} %pad_clamp_fusion), kind=kCustom, calls=%fused_computation.1 | custom fusion | bytes 22020180 | tf_op jit(solution)/shard_map/jit(_take)/gather | solution.py:64
  333.4 14.4 %convert_bitcast_fusion.1 = bf16[256,21,256]{2,0,1:T(8,128)(2,1)} fusion(bf16[21,256,1024]{2,1,0:T(8,128)(2,1)} %param.13, bf16[21,256,1024]{2,1,0:T(8,128)(2,1)} %gather_fusion.1, pred[21]{0:T(512)(128)(4,1)S(1)} %get-tuple-element.7), kind=kOutput, calls=%fused_computation.18 | convolution fusion | flops 2825453568 | bytes 24772628 | tf_op jit(solution)/shard_map/ktd,kbd->tkb/dot_general | solution.py:69
  347.9 76.9 %all-reduce.8.cloned.1.call-done = bf16[256,21,256]{2,0,1:T(8,128)(2,1)} async-done(((bf16[256,21,256]{2,0,1:T(8,128)(2,1)}), bf16[256,21,256]{2,0,1:T(8,128)(2,1)}) %all-reduce.8.cloned.1.call-update) | async-done | bytes 2752528 | tf_op jit(solution)/shard_map/psum | solution.py:72
  424.8 4.2 convert_bitcast_fusion
  429.0 2.4 copy.32
  431.4 94.7 %all_to_all.5 = bf16[256,32,256]{2,0,1:T(8,128)(2,1)S(1)} all-to-all(bf16[256,32,256]{2,0,1:T(8,128)(2,1)S(1)} %copy.32), channel_id=1, replica_groups=mesh['grp'=2,'lay'=4,'wid'=2,'rep'=2] {'lay'}, dimensions={1} | all-to-all | bytes 8388608 | tf_op jit(solution)/shard_map/all_to_all | solution.py:76
  530.3 3.3 convolution_convert_fusion
  533.7 10.5 %multiply_convert_fusion = bf16[21,256,1024]{2,1,0:T(8,128)(2,1)} fusion(f32[21]{0:T(128)S(1)} %compare_convert_fusion, bf16[21,256,1024]{2,1,0:T(8,128)(2,1)} %gather_fusion.1, pred[21]{0:T(512)(128)(4,1)S(1)} %get-tuple-element.7, bf16[21,256,256]{2,1,0:T(8,128)(2,1)} %gather_fusion, pred[21]{0:T(512)(128)(4,1)S(1)} %get-tuple-element.5), kind=kOutput, calls=%fused_computation.4 | convolution fusion | flops 2836463616 | bytes 24772734 | tf_op jit(solution)/shard_map/tkb,ktd->kbd/dot_general | solution.py:66
  546.1 5.0 all-reduce.1
  551.7 4.1 convert_element_type.90
  555.8 14.3 %reduce-scatter.5.cloned.1.call-done = bf16[21,128,1024]{2,1,0:T(8,128)(2,1)} async-done(((bf16[21,256,1024]{2,1,0:T(8,128)(2,1)}), bf16[21,128,1024]{2,1,0:T(8,128)(2,1)}) %reduce-scatter.5.cloned.1.call-update) | async-done | bytes 5505040 | tf_op jit(solution)/shard_map/reduce_scatter | solution.py:93
  570.1 8.2 %convert_element_type.94 = f32[21,128,1024]{2,1,0:T(8,128)} convert(bf16[21,128,1024]{2,1,0:T(8,128)(2,1)} %reduce-scatter.5.cloned.1.call-done) | non-fusion elementwise | flops 2752512 | bytes 16515072 | tf_op jit(solution)/shard_map/convert_element_type | solution.py:95
  (48 shorter events, 12.3 us)
Async XLA Ops:
  7.2 1.6 copy-start
  7.2 46.3 %all-reduce.6.cloned.1.call-start = ((), (), s32[]{:S(2)}) async-start(), calls=%async_computation.3 | async-start | bytes 2097152 | tf_op jit(solution)/shard_map/psum | solution.py:37
  8.8 4.5 copy-start.4
  13.2 123.3 %all-gather.3.cloned.1.call-start = ((), (), s32[]{:S(2)}) async-start(), calls=%async_computation.4 | async-start | bytes 5242880 | tf_op jit(solution)/shard_map/all_gather | solution.py:41
  13.4 40.1 %copy-start.3 = (f32[2048]{0:T(1024)S(1)}, f32[2048]{0:T(1024)}, u32[]{:S(2)}) copy-start(f32[2048]{0:T(1024)} %param.10) | copy-start | bytes 24580
  16.0 41.2 %copy-start.5 = (s32[21,3]{0,1:T(4,128)S(1)}, s32[21,3]{0,1:T(4,128)}, u32[]{:S(2)}) copy-start(s32[21,3]{0,1:T(4,128)} %param.12) | copy-start | bytes 760
  57.2 218.2 %all-reduce.10.cloned.1.call-start = ((), (), s32[]{:S(2)}) async-start(), calls=%async_computation.9 | async-start | bytes 4194304
  161.1 28.5 %copy-start.7 = (u32[32]{0:T(128)S(1)}, u32[32]{0:T(128)}, u32[]{:S(2)}) copy-start(u32[32]{0:T(128)} %constant.86) | copy-start | bytes 388
  189.6 132.9 %all-gather.5.cloned.1.call-start = ((), (), s32[]{:S(2)}) async-start(), calls=%async_computation.5 | async-start | bytes 2621440 | tf_op jit(solution)/shard_map/all_gather | solution.py:63
  277.8 147.0 %all-reduce.8.cloned.1.call-start = ((), (), s32[]{:S(2)}) async-start(), calls=%async_computation.6 | async-start | bytes 5505024 | tf_op jit(solution)/shard_map/psum | solution.py:72
  347.9 203.8 %reduce-scatter.3.cloned.1.call-start = ((), (), s32[]{:S(2)}) async-start(), calls=%async_computation.7 | async-start | bytes 6291456 | tf_op jit(solution)/shard_map/reduce_scatter | solution.py:87
  526.8 1.6 copy-start.1
  526.8 1.8 copy-start.2
  533.6 36.5 %reduce-scatter.5.cloned.1.call-start = ((), (), s32[]{:S(2)}) async-start(), calls=%async_computation.8 | async-start | bytes 16515072 | tf_op jit(solution)/shard_map/reduce_scatter | solution.py:93
  544.1 0.7 copy-start.6
Sparse Core Ops, SparseCore 0:
  13.3 40.0 all-reduce.5
  57.3 79.1 all-gather.2
  189.7 85.6 all-reduce.9
  278.0 44.4 all-gather.4
  348.0 76.8 all-reduce.7
  533.7 14.4 reduce-scatter.2
  550.6 19.4 reduce-scatter.4
where the time goes:
time: 587 us; the launch traced here: 585 us
  waiting for transfers between devices  336 us (57%)
  blocking collectives  99.7 us (17%)
  matrix products  80.6 us (14%)
  local copies, waits for them, and re-layouts  31.6 us (5%)
  other arithmetic  21.3 us (4%)
  between operations  15.6 us (3%)
    all_to_all x1, blocking collectives, local(): lax.all_to_all(outgoing, 'lay', split_axis=1, concat_axis=1, tiled=True)  94.7 us
    unnamed x8, waiting for transfers between devices  83.5 us
    all_gather x1, waiting for transfers between devices, local(): lax.all_gather(latent, 'lay', axis=1, tiled=True)  79.2 us
    psum x1, waiting for transfers between devices, local(): lax.psum(slot_error.astype(jnp.bfloat16), 'wid').astype(jnp.float32)  76.9 us
    all_gather x1, waiting for transfers between devices, local(): error_full = lax.all_gather(scaled_error, 'lay', axis=1, tiled=True)  44.6 us
    psum x1, waiting for transfers between devices, local(): lax.psum(partial_pre.astype(jnp.bfloat16), 'wid').astype(jnp.float32)  37.4 us
    dot_general x1, matrix products, local(): jnp.einsum('kl,ktd->ltd', target_hot, contrib, precision=lax.Precision.HI...  28.4 us
    dot_general x1, matrix products, local(): jnp.einsum('tkb,kbd->ktd', slot_lat, dec_weight, preferred_element_type=j...  15.3 us
  transfers between devices with their start and end apart: 7, of which 6 were waited for; matrix products, arithmetic and copies ran while one was open for 3% of the time, Pallas kernels for 0%

commit v1 on v0

v1 whole, which is shorter than its diff:
```python
import jax
import jax.numpy as jnp
from jax import lax
from jax.experimental import pallas as pl
from jax.experimental.pallas import tpu as pltpu
from jax.sharding import PartitionSpec as P

ROOT = 0.7978845608028654
CUBIC = 0.044715
MESH = pl.DeviceIdType.MESH
BF16 = jnp.bfloat16
F32 = jnp.float32


def smooth_gate(shifted):
    inside_arg = ROOT * (shifted + CUBIC * shifted * shifted * shifted)
    return 0.5 * shifted * (1.0 + jnp.tanh(inside_arg))


def gate_slope(shifted):
    inside_arg = ROOT * (shifted + CUBIC * shifted * shifted * shifted)
    tanh_part = jnp.tanh(inside_arg)
    return 0.5 * (1.0 + tanh_part) + 0.5 * shifted * (1.0 - tanh_part * tanh_part) * ROOT * (
        1.0 + 3.0 * CUBIC * shifted * shifted
    )


def loop(first, count, step):
    if count <= 4:
        for d in range(first, count):
            step(d)
    else:
        lax.fori_loop(first, count, lambda d, c: (step(d), c)[1], 0)


def others(me, count, step):
    loop(1, count, lambda d: step(lax.rem(me + d, count)))


def signal(barrier, **where):
    pl.semaphore_signal(barrier, inc=1, device_id=where, device_id_type=MESH)


def remote(src, dst, send_sem, recv_sem, **where):
    return pltpu.make_async_remote_copy(
        src_ref=src, dst_ref=dst, send_sem=send_sem, recv_sem=recv_sem, device_id=where,
        device_id_type=MESH,
    )


ANY = pl.BlockSpec(memory_space=pl.ANY)


def comm(body, args, outs, sems, cid):
    return pl.pallas_call(
        body,
        out_shape=tuple(outs),
        in_specs=[ANY] * len(args),
        out_specs=tuple([ANY] * len(outs)),
        scratch_shapes=[pltpu.SemaphoreType.DMA((s,)) for s in sems],
        compiler_params=pltpu.CompilerParams(collective_id=cid, has_side_effects=True),
        name=f"exchange_{cid}",
    )(*args)


def exchange(axis, x, out_shape, src_of, dst_of, cid):
    n = lax.axis_size(axis)

    def body(x_ref, o_ref, ssem, rsem, lsem):
        me = lax.axis_index(axis)
        barrier = pltpu.get_barrier_semaphore()
        others(me, n, lambda j: signal(barrier, **{axis: j}))
        pl.semaphore_wait(barrier, n - 1)

        def send(j):
            return remote(
                src_of(x_ref, j), dst_of(o_ref, me), ssem.at[j], rsem.at[me], **{axis: j}
            )

        def arrival(j):
            return remote(
                src_of(x_ref, me), dst_of(o_ref, j), ssem.at[j], rsem.at[j], **{axis: j}
            )

        others(me, n, lambda j: send(j).start())
        own = pltpu.make_async_copy(src_of(x_ref, me), dst_of(o_ref, me), lsem.at[0])
        own.start()
        others(me, n, lambda j: arrival(j).wait_recv())
        others(me, n, lambda j: send(j).wait_send())
        own.wait()

    return comm(body, [x], [jax.ShapeDtypeStruct(out_shape, x.dtype)], (n, n, 1), cid)[0]


def gather_latents(h, cid):
    n, w_count = lax.axis_size("lay"), lax.axis_size("wid")
    blocks, toks, width = h.shape

    def body(h_ref, o_ref, zs, zr, xs, xr, lsem):
        l, w = lax.axis_index("lay"), lax.axis_index("wid")
        barrier = pltpu.get_barrier_semaphore()
        others(l, n, lambda j: signal(barrier, lay=j))
        others(w, w_count, lambda v: signal(barrier, wid=v))
        pl.semaphore_wait(barrier, n + w_count - 2)

        def slot(j, v):
            return o_ref.at[pl.ds(j * blocks, blocks), v]

        def z_copy(j, source):
            return remote(h_ref, slot(source, w), zs.at[j], zr.at[source], lay=j)

        def x_own(v):
            return remote(h_ref, slot(l, w), xs.at[l * w_count + v], xr.at[l * w_count + w], wid=v)

        def x_copy(j, v, source):
            return remote(
                slot(j, source), slot(j, source), xs.at[j * w_count + v],
                xr.at[j * w_count + source], wid=v,
            )

        def nearest(step):
            def both(d):
                for j in (l - d, l + d):
                    @pl.when((j >= 0) & (j < n))
                    def _():
                        step(j)
            loop(1, n, both)

        others(w, w_count, lambda v: x_own(v).start())
        nearest(lambda j: z_copy(j, l).start())
        own = pltpu.make_async_copy(h_ref, slot(l, w), lsem.at[0])
        own.start()

        def forward(j):
            z_copy(j, j).wait_recv()
            others(w, w_count, lambda v: x_copy(j, v, w).start())

        nearest(forward)
        others(w, w_count, lambda v: x_own(v).wait_send())
        nearest(lambda j: z_copy(j, l).wait_send())
        nearest(lambda j: others(w, w_count, lambda v: x_copy(j, v, w).wait_send()))
        loop(0, n, lambda j: others(w, w_count, lambda v: x_copy(j, v, v).wait_recv()))
        own.wait()

    out = jax.ShapeDtypeStruct((n * blocks, w_count, toks, width), h.dtype)
    return comm(body, [h], [out], (n, n, n * w_count, n * w_count, 1), cid)[0]


def slots_and_twin(slot_err, lat, err, acts_here, cid):
    w_count, r_count = lax.axis_size("wid"), lax.axis_size("rep")
    assert r_count == 2
    slots, _, toks, width = slot_err.shape
    half = width // r_count

    def body(s_ref, l_ref, e_ref, a_ref, so_ref, lo_ref, eo_ref, ao_ref, ssem, rsem, lsem, ts, tr):
        w, r = lax.axis_index("wid"), lax.axis_index("rep")
        twin = 1 - r
        barrier = pltpu.get_barrier_semaphore()
        others(w, w_count, lambda v: signal(barrier, wid=v))
        signal(barrier, rep=twin)
        pl.semaphore_wait(barrier, w_count)

        def send(v):
            return remote(s_ref.at[:, v], so_ref.at[w], ssem.at[v], rsem.at[w], wid=v)

        def arrival(v):
            return remote(s_ref.at[:, w], so_ref.at[v], ssem.at[v], rsem.at[v], wid=v)

        others(w, w_count, lambda v: send(v).start())
        twins = [
            remote(l_ref.at[:, :, pl.ds(pl.multiple_of(twin * half, half), half)], lo_ref,
                   ts.at[0], tr.at[0], rep=twin),
            remote(e_ref, eo_ref, ts.at[1], tr.at[1], rep=twin),
            remote(a_ref, ao_ref, ts.at[2], tr.at[2], rep=twin),
        ]
        for c in twins:
            c.start()
        own = pltpu.make_async_copy(s_ref.at[:, w], so_ref.at[w], lsem.at[0])
        own.start()
        others(w, w_count, lambda v: arrival(v).wait_recv())
        others(w, w_count, lambda v: send(v).wait_send())
        own.wait()
        for c in twins:
            c.wait()

    outs = [
        jax.ShapeDtypeStruct((w_count, slots, toks, width), slot_err.dtype),
        jax.ShapeDtypeStruct(lat.shape[:2] + (half,), lat.dtype),
        jax.ShapeDtypeStruct(err.shape, err.dtype),
        jax.ShapeDtypeStruct(acts_here.shape, acts_here.dtype),
    ]
    return comm(body, [slot_err, lat, err, acts_here], outs, (w_count, w_count, 1, 3, 3), cid)


def gather_pre_grad(pg, cid):
    w_count, r_count = lax.axis_size("wid"), lax.axis_size("rep")
    _, toks, columns = pg.shape

    def body(p_ref, o_ref, ssem, rsem, lsem):
        w, r = lax.axis_index("wid"), lax.axis_index("rep")
        barrier = pltpu.get_barrier_semaphore()

        def peers(step):
            others(w, w_count, lambda v: loop(0, r_count, lambda q: step(v, q)))
            others(r, r_count, lambda q: step(w, q))

        peers(lambda v, q: signal(barrier, wid=v, rep=q))
        pl.semaphore_wait(barrier, w_count * r_count - 1)

        def send(v, q):
            return remote(p_ref.at[q], o_ref.at[r, w], ssem.at[q * w_count + v],
                          rsem.at[r * w_count + w], wid=v, rep=q)

        def arrival(v, q):
            return remote(p_ref.at[q], o_ref.at[q, v], ssem.at[q * w_count + v],
                          rsem.at[q * w_count + v], wid=v, rep=q)

        peers(lambda v, q: send(v, q).start())
        own = pltpu.make_async_copy(p_ref.at[r], o_ref.at[r, w], lsem.at[0])
        own.start()
        peers(lambda v, q: arrival(v, q).wait_recv())
        peers(lambda v, q: send(v, q).wait_send())
        own.wait()

    out = jax.ShapeDtypeStruct((r_count, w_count, toks, columns), pg.dtype)
    total = w_count * r_count
    return comm(body, [pg], [out], (total, total, 1), cid)[0]


def slot_call(body, tables, args, in_specs, out_shape, out_spec, scratch, flops, name):
    moved = sum(a.size * a.dtype.itemsize for a in args) + out_shape.size * out_shape.dtype.itemsize
    return pl.pallas_call(
        body,
        out_shape=out_shape,
        grid_spec=pltpu.PrefetchScalarGridSpec(
            num_scalar_prefetch=len(tables), grid=(tables[0].shape[0],), in_specs=in_specs,
            out_specs=out_spec, scratch_shapes=scratch,
        ),
        compiler_params=pltpu.CompilerParams(vmem_limit_bytes=48 * 1024 * 1024),
        cost_estimate=pl.CostEstimate(flops=flops, bytes_accessed=moved, transcendentals=0),
        name=name,
    )(*tables, *args)


def decode(ids, tgt, valid, lat, dec_weight, layers):
    slots, block, width = dec_weight.shape
    toks = lat.shape[1]

    def body(i_ref, t_ref, v_ref, lat_ref, w_ref, o_ref, acc):
        k = pl.program_id(0)

        @pl.when(k == 0)
        def _():
            acc[...] = jnp.zeros_like(acc)

        @pl.when(v_ref[k] > 0)
        def _():
            acc[t_ref[k]] += jnp.dot(lat_ref[0], w_ref[0], preferred_element_type=F32)

        @pl.when(k == slots - 1)
        def _():
            o_ref[...] = acc[...].astype(o_ref.dtype)

    return slot_call(
        body, (ids, tgt, valid), (lat, dec_weight),
        [pl.BlockSpec((1, toks, block), lambda k, i, t, v: (i[k], 0, 0)),
         pl.BlockSpec((1, block, width), lambda k, i, t, v: (k, 0, 0))],
        jax.ShapeDtypeStruct((layers, toks, width), BF16),
        pl.BlockSpec((layers, toks, width), lambda k, i, t, v: (0, 0, 0)),
        [pltpu.VMEM((layers, toks, width), F32)], 2 * slots * toks * block * width, "decode",
    )


def slot_errors(tgt, err, dec_weight):
    slots, block, width = dec_weight.shape
    layers, toks, _ = err.shape

    def body(t_ref, e_ref, w_ref, o_ref):
        k = pl.program_id(0)
        o_ref[0] = lax.dot_general(
            e_ref[t_ref[k]], w_ref[0], (((1,), (1,)), ((), ())), preferred_element_type=F32
        ).astype(o_ref.dtype)

    return slot_call(
        body, (tgt,), (err, dec_weight),
        [pl.BlockSpec((layers, toks, width), lambda k, t: (0, 0, 0)),
         pl.BlockSpec((1, block, width), lambda k, t: (k, 0, 0))],
        jax.ShapeDtypeStruct((slots, toks, block), BF16),
        pl.BlockSpec((1, toks, block), lambda k, t: (k, 0, 0)),
        [], 2 * slots * toks * block * width, "slot_errors",
    )


def combine(ids, valid, parts, blocks_total):
    w_count, slots, toks, block = parts.shape

    def body(i_ref, v_ref, p_ref, o_ref, acc):
        k = pl.program_id(0)

        @pl.when(k == 0)
        def _():
            acc[...] = jnp.zeros_like(acc)

        @pl.when(v_ref[k] > 0)
        def _():
            acc[i_ref[k]] += jnp.sum(p_ref[:, 0].astype(F32), axis=0)

        @pl.when(k == slots - 1)
        def _():
            o_ref[...] = acc[...].astype(o_ref.dtype)

    return slot_call(
        body, (ids, valid), (parts,),
        [pl.BlockSpec((w_count, 1, toks, block), lambda k, i, v: (0, k, 0, 0))],
        jax.ShapeDtypeStruct((blocks_total, toks, block), BF16),
        pl.BlockSpec((blocks_total, toks, block), lambda k, i, v: (0, 0, 0)),
        [pltpu.VMEM((blocks_total, toks, block), F32)], w_count * slots * toks * block, "combine",
    )


def decoder_grads(ids, tgt, valid, rep, lat, lat_twin, err, err_twin, slots):
    layers, toks, width = err.shape
    half = lat_twin.shape[2]

    def body(i_ref, t_ref, v_ref, r_ref, l_ref, lt_ref, e_ref, et_ref, o_ref):
        k = pl.program_id(0)
        over = (((0,), (0,)), ((), ()))

        @pl.when(v_ref[k] > 0)
        def _():
            t = t_ref[k]
            o_ref[0] = lax.dot_general(
                l_ref[0], e_ref[t], over, preferred_element_type=F32
            ) + lax.dot_general(lt_ref[0], et_ref[t], over, preferred_element_type=F32)

        @pl.when(v_ref[k] == 0)
        def _():
            o_ref[...] = jnp.zeros_like(o_ref)

    return slot_call(
        body, (ids, tgt, valid, rep), (lat, lat_twin, err, err_twin),
        [pl.BlockSpec((1, toks, half), lambda k, i, t, v, r: (i[k], 0, r[0])),
         pl.BlockSpec((1, toks, half), lambda k, i, t, v, r: (i[k], 0, 0)),
         pl.BlockSpec((layers, toks, width), lambda k, i, t, v, r: (0, 0, 0)),
         pl.BlockSpec((layers, toks, width), lambda k, i, t, v, r: (0, 0, 0))],
        jax.ShapeDtypeStruct((slots, half, width), F32),
        pl.BlockSpec((1, half, width), lambda k, i, t, v, r: (k, 0, 0)),
        [], 4 * slots * toks * half * width, "decoder_grads",
    )


def local(acts, targets, enc_weight, enc_bias, gate_mask, dec_list, dec_weight):
    layers, tok_rows, width_part = acts.shape
    lat_dev = enc_weight.shape[1]
    slots, block, _ = dec_weight.shape
    per_dev = lat_dev // block
    n, w_count, r_count = lax.axis_size("lay"), lax.axis_size("wid"), lax.axis_size("rep")
    lay, wid, rep = lax.axis_index("lay"), lax.axis_index("wid"), lax.axis_index("rep")
    lat_total = lat_dev * n
    blocks_total = lat_total // block
    latents_layer = lat_total // layers
    blocks_layer = latents_layer // block
    toks = tok_rows // w_count
    rows = tok_rows // n

    tgt = dec_list[:, 1]
    valid = (tgt >= 0).astype(jnp.int32)
    ids = jnp.maximum(dec_list[:, 0] * blocks_layer + dec_list[:, 2], 0)
    tgt = jnp.maximum(tgt, 0)

    here = lax.dynamic_index_in_dim(acts, lay * lat_dev // latents_layer, 0, keepdims=False)
    partial = jnp.dot(here, enc_weight, preferred_element_type=F32).astype(BF16)
    parts = exchange(
        "wid", partial.reshape(w_count, toks, lat_dev), (w_count, toks, lat_dev),
        lambda x, j: x.at[j], lambda o, j: o.at[j], 0,
    )
    shifted = jnp.sum(parts.astype(F32), axis=0) + enc_bias[None, :]
    shifted = shifted.reshape(toks, per_dev, block).transpose(1, 0, 2)
    keep = lax.dynamic_slice_in_dim(gate_mask, wid * toks, toks, 0).astype(F32).T[:, :, None]
    latent = (smooth_gate(shifted) * keep).astype(BF16)
    lat = gather_latents(latent, 1).reshape(blocks_total, tok_rows, block)

    recon_part = decode(ids, tgt, valid, lat, dec_weight, layers)
    recon_in = exchange(
        "lay", recon_part.reshape(layers, n, rows, width_part), (n, layers, rows, width_part),
        lambda x, j: x.at[:, j], lambda o, j: o.at[j], 2,
    )
    recon = jnp.sum(recon_in.astype(F32), axis=0)
    own_target = lax.dynamic_slice_in_dim(targets, lay * rows, rows, 1)
    scale = float(tok_rows * r_count) ** (-0.5)
    own_err = ((recon - own_target.astype(F32)) * scale).astype(BF16)
    err = exchange(
        "lay", own_err, (layers, n, rows, width_part),
        lambda x, j: x, lambda o, j: o.at[:, j], 3,
    ).reshape(layers, tok_rows, width_part)

    slot_err = slot_errors(tgt, err, dec_weight).reshape(slots, w_count, toks, block)
    slot_in, lat_twin, err_twin, acts_twin = slots_and_twin(slot_err, lat, err, here, 4)
    outgoing = combine(ids, valid, slot_in, blocks_total)
    incoming = exchange(
        "lay", outgoing.reshape(n, per_dev, toks, block), (n, per_dev, toks, block),
        lambda x, j: x.at[j], lambda o, j: o.at[j], 5,
    )
    dec_out = decoder_grads(
        ids, tgt, valid, rep.reshape(1).astype(jnp.int32), lat, lat_twin, err, err_twin, slots
    )
    latent_error = jnp.sum(incoming.astype(F32), axis=0)
    pre_grad = (latent_error * keep * gate_slope(shifted)).astype(BF16)
    columns = lat_dev // r_count
    pre_grad = pre_grad.transpose(1, 0, 2).reshape(toks, r_count, columns).transpose(1, 0, 2)
    pre_all = gather_pre_grad(pre_grad, 6).reshape(r_count, tok_rows, columns)

    mine = lax.dynamic_index_in_dim(pre_all, rep, 0, keepdims=False)
    theirs = lax.dynamic_index_in_dim(pre_all, 1 - rep, 0, keepdims=False)
    over = (((0,), (0,)), ((), ()))
    enc_out = lax.dot_general(
        jnp.concatenate([here, acts_twin], 0), jnp.concatenate([mine, theirs], 0), over,
        preferred_element_type=F32,
    )
    bias_out = jnp.sum(pre_all.astype(F32), axis=(0, 1))
    return (enc_out, bias_out, dec_out)


def solution(mesh):
    return jax.shard_map(
        local,
        mesh=mesh,
        in_specs=(
            P(None, ("grp", "rep"), "wid"),
            P(None, ("grp", "rep"), "wid"),
            P("wid", "lay"),
            P("lay"),
            P(("grp", "rep"), "lay"),
            P("lay", None),
            P("lay", None, "wid"),
        ),
        out_specs=(
            P(("grp", "wid"), ("lay", "rep")),
            P(("grp", "lay", "rep")),
            P(("grp", "lay"), "rep", "wid"),
        ),
        check_vma=False,
    )
```

time: 587 us -> 383 us (0.65)
  Pallas kernels: 0 us -> 342 us
  waiting for transfers between devices: 336 us -> 0 us
  blocking collectives: 99.7 us -> 0 us
  matrix products: 80.6 us -> 7.95 us
  local copies, waits for them, and re-layouts: 31.6 us -> 14.1 us
  between operations: 15.6 us -> 0.87 us
  other arithmetic: 21.3 us -> 15.4 us
    pallas_call x0 -> x11, Pallas kernels: none -> 342 us  [the longest x7 291 us: comm(): pl.pallas_call(body, out_shape=tuple(outs), in_specs=[ANY] * len(args), o...]
    all_gather x2 -> x0, waiting for transfers between devices: 124 us -> none  [the longest x1 79.2 us: local(): lax.all_gather(latent, 'lay', axis=1, tiled=True)]
    psum x2 -> x0, waiting for transfers between devices: 114 us -> none  [the longest x1 76.9 us: local(): lax.psum(slot_error.astype(jnp.bfloat16), 'wid').astype(jnp.float32)]
    all_to_all x1 -> x0, blocking collectives: 94.7 us -> none  [local(): lax.all_to_all(outgoing, 'lay', split_axis=1, concat_axis=1, tiled=True)]
    unnamed x8 -> x0, waiting for transfers between devices: 83.5 us -> none
    dot_general x7 -> x2, matrix products: 80.6 us -> 7.95 us  [the longest x1 4.62 us: local(): partial = jnp.dot(here, enc_weight, preferred_element_type=F32).astype(BF16)]
    reduce_scatter x2 -> x0, waiting for transfers between devices: 14.3 us -> none  [the longest x1 14.3 us: local(): lax.psum_scatter(dec_grad.astype(jnp.bfloat16), 'rep', scatter_dimension=...]
    convert_element_type x7 -> x5, other arithmetic: 19 us -> 6.28 us  [the longest x1 2.02 us: local(): own_err = ((recon - own_target.astype(F32)) * scale).astype(BF16)]
  transfers between devices with their start and end apart: 7 -> 0, of which waited for: 6 -> 0; matrix products, arithmetic and copies ran while one was open for 3% -> 0% of each run, Pallas kernels for 0% -> 0%
where the time goes in v1:
time: 383 us; the launch traced here: 380 us
  Pallas kernels  342 us (89%)
  other arithmetic  15.4 us (4%)
  local copies, waits for them, and re-layouts  14.1 us (4%)
  matrix products  7.95 us (2%)
    pallas_call x7, Pallas kernels, comm(): pl.pallas_call(body, out_shape=tuple(outs), in_specs=[ANY] * len(args), o...  291 us
    pallas_call x4, Pallas kernels, slot_call(): pl.pallas_call(body, out_shape=out_shape, grid_spec=pltpu.PrefetchScalarG...  51.6 us
    unnamed x24, local copies, waits for them, and re-layouts  9.14 us

profile of v1, /device:TPU:15, one launch (start us, length us, event | category | flops | bytes accessed | tf_op | source)
XLA Modules:
  0.0 380.5 jit_solution(11667053024671377138)
XLA Ops:
  4.4 4.6 %convolution_convert_fusion = bf16[256,2048]{1,0:T(8,128)(2,1)} fusion(bf16[256,1024]{1,0:T(8,128)(2,1)S(1)} %dynamic-slice_bitcast_fusion.2.a_ref, bf16[1024,2048]{1,0:T(8,128)(2,1)} %param.9), kind=kOutput, calls=%fused_computation.2 | convolution fusion | flops 1074266112 | bytes 5767168 | tf_op jit(solution)/shard_map/dot_general | solution.py:372
  9.1 17.3 %exchange_0.1 = bf16[2,128,2048]{2,1,0:T(8,128)(2,1)} custom-call(bf16[2,128,2048]{2,1,0:T(8,128)(2,1)} %bitcast.49), custom_call_target="tpu_custom_call" | custom-call | tf_op jit(solution)/shard_map/exchange_0/pallas_call | solution.py:55
  26.3 1.5 convert_reduce_fusion.3
  29.7 47.0 %exchange_1.1 = bf16[32,2,128,256]{3,2,1,0:T(8,128)(2,1)} custom-call(bf16[8,128,256]{2,1,0:T(8,128)(2,1)} %fusion.5.h_ref), custom_call_target="tpu_custom_call" | custom-call | tf_op jit(solution)/shard_map/exchange_1/pallas_call | solution.py:55
  76.7 16.6 %decode.1 = bf16[4,256,1024]{2,1,0:T(8,128)(2,1)S(1)} custom-call(s32[21]{0:T(128)S(1)} %get-tuple-element.13.i_ref, s32[21]{0:T(128)S(1)} %get-tuple-element.14.t_ref, s32[21]{0:T(128)S(1)} %fusion.20.v_ref, bf16[32,256,256]{2,1,0:T(8,128)(2,1)} %bitcast.42, bf16[21,256,1024]{2,1,0:T(8,128)(2,1)} %w_ref.3), custom_call_target="tpu_custom_call" | custom-call | flops 2818572288 | bytes 17301504 | tf_op jit(solution)/shard_map/decode/pallas_call | solution.py:232
  94.6 72.4 %exchange_2.1 = bf16[4,4,64,1024]{3,2,1,0:T(8,128)(2,1)} custom-call(bf16[4,4,64,1024]{3,2,1,0:T(8,128)(2,1)} %bitcast.41), custom_call_target="tpu_custom_call" | custom-call | tf_op jit(solution)/shard_map/exchange_2/pallas_call | solution.py:55
  167.0 2.1 convert_reduce_fusion.1
  169.2 2.0 multiply_convert_fusion.x_ref
  171.2 47.2 %exchange_3.1 = bf16[4,4,64,1024]{3,2,1,0:T(8,128)(2,1)} custom-call(bf16[4,64,1024]{2,1,0:T(8,128)(2,1)} %multiply_convert_fusion.x_ref), custom_call_target="tpu_custom_call" | custom-call | tf_op jit(solution)/shard_map/exchange_3/pallas_call | solution.py:55
  218.4 1.6 copy-done.2
  220.0 16.0 %slot_errors.1 = bf16[21,256,256]{2,1,0:T(8,128)(2,1)S(1)} custom-call(s32[21]{0:T(128)S(1)} %get-tuple-element.14.t_ref, bf16[4,256,1024]{2,1,0:T(8,128)(2,1)S(1)} %bitcast.37, bf16[21,256,1024]{2,1,0:T(8,128)(2,1)} %w_ref.3), custom_call_target="tpu_custom_call" | custom-call | flops 2818572288 | bytes 15859712 | tf_op jit(solution)/shard_map/slot_errors/pallas_call | solution.py:232
  236.0 1.5 copy-done.4
  237.5 44.2 %exchange_4.1 = (bf16[2,21,128,256]{3,2,1,0:T(8,128)(2,1)}, bf16[32,256,128]{2,1,0:T(8,128)(2,1)}, bf16[4,256,1024]{2,1,0:T(8,128)(2,1)}, bf16[256,1024]{1,0:T(8,128)(2,1)}) custom-call(bf16[21,2,128,256]{3,2,1,0:T(8,128)(2,1)} %bitcast.39, bf16[32,256,256]{2,1,0:T(8,128)(2,1)} %bitcast.43, bf16[4,256,1024]{2,1,0:T(8,128)(2,1)} %bitcast.36, ...), custom_call_target="tpu_custom_call" | custom-call | tf_op jit(solution)/shard_map/exchange_4/pallas_call | solution.py:55
  281.8 1.8 copy-done.7
  283.5 2.2 combine.1
  287.1 47.1 %exchange_5.1 = bf16[4,8,128,256]{3,2,1,0:T(8,128)(2,1)} custom-call(bf16[4,8,128,256]{3,2,1,0:T(8,128)(2,1)} %bitcast.40), custom_call_target="tpu_custom_call" | custom-call | tf_op jit(solution)/shard_map/exchange_5/pallas_call | solution.py:55
  334.2 2.0 convert_reduce_fusion
  336.3 1.5 fusion.12
  337.8 1.3 copy.15
  340.2 1.6 copy-done.8
  341.8 16.8 %decoder_grads.1 = f32[21,128,1024]{2,1,0:T(8,128)} custom-call(s32[21]{0:T(128)S(1)} %get-tuple-element.13.i_ref, s32[21]{0:T(128)S(1)} %get-tuple-element.14.t_ref, s32[21]{0:T(128)S(1)} %fusion.20.v_ref, s32[1]{0:T(128)} %bitcast.19.r_ref, bf16[32,256,256]{2,1,0:T(8,128)(2,1)} %bitcast.44, bf16[32,256,128]{2,1,0:T(8,128)(2,1)S(1)} %copy-done.8, ...), custom_call_target="tpu_custom_call" | custom-call | flops 2818572288 | bytes 21495808 | tf_op jit(solution)/shard_map/decoder_grads/pallas_call | solution.py:232
  358.5 15.3 %exchange_6.1 = bf16[2,2,128,1024]{3,2,1,0:T(8,128)(2,1)} custom-call(bf16[2,128,1024]{2,1,0:T(8,128)(2,1)} %bitcast.47), custom_call_target="tpu_custom_call" | custom-call | tf_op jit(solution)/shard_map/exchange_6/pallas_call | solution.py:55
  373.8 2.0 convert_reduce_fusion.2
  377.1 3.3 fusion.13
  (31 shorter events, 10.6 us)
Async XLA Ops:
  0.6 3.8 copy-start
  4.4 4.6 %copy-start.9 = (bf16[256,1024]{1,0:T(8,128)(2,1)}, bf16[256,1024]{1,0:T(8,128)(2,1)S(1)}, u32[]{:S(2)}) copy-start(bf16[256,1024]{1,0:T(8,128)(2,1)S(1)} %dynamic-slice_bitcast_fusion.2.a_ref) | copy-start | bytes 1572868
  93.3 1.3 copy-start.6
  218.4 1.6 copy-start.2
  236.0 1.5 copy-start.4
  281.8 1.8 copy-start.7
  285.7 1.3 copy-start.5
  336.3 3.9 %copy-start.3 = (bf16[4,4,64,1024]{3,2,1,0:T(8,128)(2,1)S(1)}, bf16[4,4,64,1024]{3,2,1,0:T(8,128)(2,1)}, u32[]{:S(2)}) copy-start(bf16[4,4,64,1024]{3,2,1,0:T(8,128)(2,1)} %exchange_3.1) | copy-start | bytes 6291460
  340.2 1.6 copy-start.8
  358.5 18.6 %copy-start.10 = (bf16[256,1024]{1,0:T(8,128)(2,1)S(1)}, bf16[256,1024]{1,0:T(8,128)(2,1)}, u32[]{:S(2)}) copy-start(bf16[256,1024]{1,0:T(8,128)(2,1)} %copy-done.9) | copy-start | bytes 1572868
  358.5 18.6 %copy-start.11 = (bf16[256,1024]{1,0:T(8,128)(2,1)S(1)}, bf16[256,1024]{1,0:T(8,128)(2,1)}, u32[]{:S(2)}) copy-start(bf16[256,1024]{1,0:T(8,128)(2,1)} %get-tuple-element.7) | copy-start | bytes 1572868
  377.1 3.4 copy-start.1

commit v2 on v1

v2 whole, which is shorter than its diff:
```python
import jax
import jax.numpy as jnp
from jax import lax
from jax.experimental import pallas as pl
from jax.experimental.pallas import tpu as pltpu
from jax.sharding import PartitionSpec as P

ROOT = 0.7978845608028654
CUBIC = 0.044715
MESH = pl.DeviceIdType.MESH
BF16 = jnp.bfloat16
F32 = jnp.float32


def smooth_gate(shifted):
    inside_arg = ROOT * (shifted + CUBIC * shifted * shifted * shifted)
    return 0.5 * shifted * (1.0 + jnp.tanh(inside_arg))


def gate_slope(shifted):
    inside_arg = ROOT * (shifted + CUBIC * shifted * shifted * shifted)
    tanh_part = jnp.tanh(inside_arg)
    return 0.5 * (1.0 + tanh_part) + 0.5 * shifted * (1.0 - tanh_part * tanh_part) * ROOT * (
        1.0 + 3.0 * CUBIC * shifted * shifted
    )


def loop(first, count, step):
    if count <= 4:
        for d in range(first, count):
            step(d)
    else:
        lax.fori_loop(first, count, lambda d, c: (step(d), c)[1], 0)


def others(me, count, step):
    loop(1, count, lambda d: step(lax.rem(me + d, count)))


def signal(barrier, **where):
    pl.semaphore_signal(barrier, inc=1, device_id=where, device_id_type=MESH)


def remote(src, dst, send_sem, recv_sem, **where):
    return pltpu.make_async_remote_copy(
        src_ref=src, dst_ref=dst, send_sem=send_sem, recv_sem=recv_sem, device_id=where,
        device_id_type=MESH,
    )


ANY = pl.BlockSpec(memory_space=pl.ANY)


def bounce(src, dst, held, sem):
    into = pltpu.make_async_copy(src, held, sem)
    into.start()
    into.wait()
    out = pltpu.make_async_copy(held, dst, sem)
    out.start()
    return out


def nearest(l, n, step):
    def both(d):
        for j in (l - d, l + d):

            @pl.when((j >= 0) & (j < n))
            def _():
                step(j)

    loop(1, n, both)


def line_gather(l, n, src, slot, send_sem, recv_sem, arrived):
    def own(step):
        @pl.when(l < n - 1)
        def _():
            step(remote(src, slot(l), send_sem.at[l], recv_sem.at[l], lay=l + 1))

        @pl.when(l > 0)
        def _():
            step(remote(src, slot(l), send_sem.at[n], recv_sem.at[l], lay=l - 1))

    def hop(j, step):
        @pl.when((j < l) & (l < n - 1))
        def _():
            step(remote(slot(j), slot(j), send_sem.at[j], recv_sem.at[j], lay=l + 1))

        @pl.when((j > l) & (l > 0))
        def _():
            step(remote(slot(j), slot(j), send_sem.at[j], recv_sem.at[j], lay=l - 1))

    def take(j):
        remote(slot(j), slot(j), send_sem.at[j], recv_sem.at[j], lay=j).wait_recv()
        hop(j, lambda c: c.start())
        arrived(j)

    def finish():
        own(lambda c: c.wait_send())
        nearest(l, n, lambda j: hop(j, lambda c: c.wait_send()))

    own(lambda c: c.start())
    return lambda: nearest(l, n, take), finish


def comm(body, args, outs, sems, cid, held=()):
    return pl.pallas_call(
        body,
        out_shape=tuple(outs),
        in_specs=[ANY] * len(args),
        out_specs=tuple([ANY] * len(outs)),
        scratch_shapes=[pltpu.SemaphoreType.DMA((s,)) for s in sems] + [pltpu.VMEM(*h) for h in held],
        compiler_params=pltpu.CompilerParams(collective_id=cid, has_side_effects=True),
        name=f"exchange_{cid}",
    )(*args)


def exchange(axis, x, out_shape, held_shape, src_of, dst_of, cid):
    n = lax.axis_size(axis)

    def body(x_ref, o_ref, ssem, rsem, lsem, held):
        me = lax.axis_index(axis)
        barrier = pltpu.get_barrier_semaphore()
        others(me, n, lambda j: signal(barrier, **{axis: j}))
        pl.semaphore_wait(barrier, n - 1)

        def send(j):
            return remote(
                src_of(x_ref, j), dst_of(o_ref, me), ssem.at[j], rsem.at[me], **{axis: j}
            )

        def arrival(j):
            return remote(
                src_of(x_ref, me), dst_of(o_ref, j), ssem.at[j], rsem.at[j], **{axis: j}
            )

        others(me, n, lambda j: send(j).start())
        own = bounce(src_of(x_ref, me), dst_of(o_ref, me), held, lsem.at[0])
        others(me, n, lambda j: arrival(j).wait_recv())
        others(me, n, lambda j: send(j).wait_send())
        own.wait()

    return comm(
        body, [x], [jax.ShapeDtypeStruct(out_shape, x.dtype)], (n, n, 1), cid,
        [(held_shape, x.dtype)],
    )[0]


def gather_errors(e, cid):
    n = lax.axis_size("lay")

    def body(e_ref, o_ref, zs, zr, lsem, held):
        l = lax.axis_index("lay")
        barrier = pltpu.get_barrier_semaphore()
        others(l, n, lambda j: signal(barrier, lay=j))
        pl.semaphore_wait(barrier, n - 1)
        take, finish = line_gather(
            l, n, e_ref, lambda j: o_ref.at[:, j], zs, zr, lambda j: None
        )
        own = bounce(e_ref, o_ref.at[:, l], held, lsem.at[0])
        take()
        finish()
        own.wait()

    out = jax.ShapeDtypeStruct((e.shape[0], n) + e.shape[1:], e.dtype)
    return comm(body, [e], [out], (n + 1, n, 1), cid, [(e.shape, e.dtype)])[0]


def gather_latents(h, cid):
    n, w_count = lax.axis_size("lay"), lax.axis_size("wid")
    blocks, toks, width = h.shape

    def body(h_ref, o_ref, zs, zr, xs, xr, lsem, held):
        l, w = lax.axis_index("lay"), lax.axis_index("wid")
        barrier = pltpu.get_barrier_semaphore()
        others(l, n, lambda j: signal(barrier, lay=j))
        others(w, w_count, lambda v: signal(barrier, wid=v))
        pl.semaphore_wait(barrier, n + w_count - 2)

        def slot(j, v):
            return o_ref.at[pl.ds(j * blocks, blocks), v]

        def x_own(v):
            return remote(h_ref, slot(l, w), xs.at[l * w_count + v], xr.at[l * w_count + w], wid=v)

        def x_copy(j, v, source):
            return remote(
                slot(j, source), slot(j, source), xs.at[j * w_count + v],
                xr.at[j * w_count + source], wid=v,
            )

        take, finish = line_gather(
            l, n, h_ref, lambda j: slot(j, w), zs, zr,
            lambda j: others(w, w_count, lambda v: x_copy(j, v, w).start()),
        )
        others(w, w_count, lambda v: x_own(v).start())
        own = bounce(h_ref, slot(l, w), held, lsem.at[0])
        take()
        finish()
        others(w, w_count, lambda v: x_own(v).wait_send())
        nearest(l, n, lambda j: others(w, w_count, lambda v: x_copy(j, v, w).wait_send()))
        loop(0, n, lambda j: others(w, w_count, lambda v: x_copy(j, v, v).wait_recv()))
        own.wait()

    out = jax.ShapeDtypeStruct((n * blocks, w_count, toks, width), h.dtype)
    return comm(
        body, [h], [out], (n + 1, n, n * w_count, n * w_count, 1), cid, [(h.shape, h.dtype)]
    )[0]


def slots_and_twin(slot_err, lat, err, acts_here, cid):
    w_count, r_count = lax.axis_size("wid"), lax.axis_size("rep")
    assert r_count == 2
    slots, _, toks, width = slot_err.shape
    half = width // r_count

    def body(s_ref, l_ref, e_ref, a_ref, so_ref, lo_ref, eo_ref, ao_ref, ssem, rsem, lsem, ts, tr,
             held, held_acts):
        w, r = lax.axis_index("wid"), lax.axis_index("rep")
        twin = 1 - r
        barrier = pltpu.get_barrier_semaphore()
        others(w, w_count, lambda v: signal(barrier, wid=v))
        signal(barrier, rep=twin)
        pl.semaphore_wait(barrier, w_count)

        def send(v):
            return remote(s_ref.at[:, v], so_ref.at[w], ssem.at[v], rsem.at[w], wid=v)

        def arrival(v):
            return remote(s_ref.at[:, w], so_ref.at[v], ssem.at[v], rsem.at[v], wid=v)

        others(w, w_count, lambda v: send(v).start())
        twins = [
            remote(l_ref.at[:, :, pl.ds(pl.multiple_of(twin * half, half), half)], lo_ref,
                   ts.at[0], tr.at[0], rep=twin),
            remote(e_ref, eo_ref, ts.at[1], tr.at[1], rep=twin),
            remote(a_ref, ao_ref.at[r], ts.at[2], tr.at[2], rep=twin),
        ]
        for c in twins:
            c.start()
        own = bounce(s_ref.at[:, w], so_ref.at[w], held, lsem.at[0])
        own_acts = bounce(a_ref, ao_ref.at[r], held_acts, lsem.at[1])
        others(w, w_count, lambda v: arrival(v).wait_recv())
        others(w, w_count, lambda v: send(v).wait_send())
        own.wait()
        own_acts.wait()
        for c in twins:
            c.wait()

    outs = [
        jax.ShapeDtypeStruct((w_count, slots, toks, width), slot_err.dtype),
        jax.ShapeDtypeStruct(lat.shape[:2] + (half,), lat.dtype),
        jax.ShapeDtypeStruct(err.shape, err.dtype),
        jax.ShapeDtypeStruct((r_count,) + acts_here.shape, acts_here.dtype),
    ]
    return comm(body, [slot_err, lat, err, acts_here], outs, (w_count, w_count, 2, 3, 3), cid,
                [((slots, toks, width), slot_err.dtype), (acts_here.shape, acts_here.dtype)])


def gather_pre_grad(pg, cid):
    w_count, r_count = lax.axis_size("wid"), lax.axis_size("rep")
    _, toks, columns = pg.shape

    def body(p_ref, o_ref, ssem, rsem, lsem, held):
        w, r = lax.axis_index("wid"), lax.axis_index("rep")
        barrier = pltpu.get_barrier_semaphore()

        def peers(step):
            others(w, w_count, lambda v: loop(0, r_count, lambda q: step(v, q)))
            others(r, r_count, lambda q: step(w, q))

        peers(lambda v, q: signal(barrier, wid=v, rep=q))
        pl.semaphore_wait(barrier, w_count * r_count - 1)

        def send(v, q):
            return remote(p_ref.at[q], o_ref.at[r, w], ssem.at[q * w_count + v],
                          rsem.at[r * w_count + w], wid=v, rep=q)

        def arrival(v, q):
            return remote(p_ref.at[q], o_ref.at[q, v], ssem.at[q * w_count + v],
                          rsem.at[q * w_count + v], wid=v, rep=q)

        peers(lambda v, q: send(v, q).start())
        own = bounce(p_ref.at[r], o_ref.at[r, w], held, lsem.at[0])
        peers(lambda v, q: arrival(v, q).wait_recv())
        peers(lambda v, q: send(v, q).wait_send())
        own.wait()

    out = jax.ShapeDtypeStruct((r_count, w_count, toks, columns), pg.dtype)
    total = w_count * r_count
    return comm(
        body, [pg], [out], (total, total, 1), cid, [((toks, columns), pg.dtype)]
    )[0]


def group_of(slots):
    return 3 if slots % 3 == 0 else 1


def slot_call(body, tables, args, in_specs, out_shape, out_spec, scratch, flops, name, grid):
    moved = sum(a.size * a.dtype.itemsize for a in args) + out_shape.size * out_shape.dtype.itemsize
    return pl.pallas_call(
        body,
        out_shape=out_shape,
        grid_spec=pltpu.PrefetchScalarGridSpec(
            num_scalar_prefetch=len(tables), grid=(grid,), in_specs=in_specs,
            out_specs=out_spec, scratch_shapes=scratch,
        ),
        compiler_params=pltpu.CompilerParams(vmem_limit_bytes=62 * 1024 * 1024),
        cost_estimate=pl.CostEstimate(flops=flops, bytes_accessed=moved, transcendentals=0),
        name=name,
    )(*tables, *args)


def decode(ids, tgt, valid, lat, dec_weight, layers):
    slots, block, width = dec_weight.shape
    blocks, toks, _ = lat.shape
    g = group_of(slots)

    def body(i_ref, t_ref, v_ref, lat_ref, w_ref, o_ref, acc):
        step = pl.program_id(0)

        @pl.when(step == 0)
        def _():
            acc[...] = jnp.zeros_like(acc)

        for i in range(g):
            k = step * g + i

            @pl.when(v_ref[k] > 0)
            def _():
                acc[t_ref[k]] += jnp.dot(
                    lat_ref[i_ref[k]], w_ref[i], preferred_element_type=F32
                )

        @pl.when(step == slots // g - 1)
        def _():
            o_ref[...] = acc[...].astype(o_ref.dtype)

    return slot_call(
        body, (ids, tgt, valid), (lat, dec_weight),
        [pl.BlockSpec((blocks, toks, block), lambda k, i, t, v: (0, 0, 0)),
         pl.BlockSpec((g, block, width), lambda k, i, t, v: (k, 0, 0))],
        jax.ShapeDtypeStruct((layers, toks, width), BF16),
        pl.BlockSpec((layers, toks, width), lambda k, i, t, v: (0, 0, 0)),
        [pltpu.VMEM((layers, toks, width), F32)], 2 * slots * toks * block * width, "decode",
        slots // g,
    )


def slot_errors(tgt, err, dec_weight):
    slots, block, width = dec_weight.shape
    layers, toks, _ = err.shape
    g = group_of(slots)

    def body(t_ref, e_ref, w_ref, o_ref):
        for i in range(g):
            k = pl.program_id(0) * g + i
            o_ref[i] = lax.dot_general(
                e_ref[t_ref[k]], w_ref[i], (((1,), (1,)), ((), ())), preferred_element_type=F32
            ).astype(o_ref.dtype)

    return slot_call(
        body, (tgt,), (err, dec_weight),
        [pl.BlockSpec((layers, toks, width), lambda k, t: (0, 0, 0)),
         pl.BlockSpec((g, block, width), lambda k, t: (k, 0, 0))],
        jax.ShapeDtypeStruct((slots, toks, block), BF16),
        pl.BlockSpec((g, toks, block), lambda k, t: (k, 0, 0)),
        [], 2 * slots * toks * block * width, "slot_errors", slots // g,
    )


def combine(ids, valid, parts, blocks_total):
    w_count, slots, toks, block = parts.shape

    g = slots // 3 if slots % 3 == 0 else 1

    def body(i_ref, v_ref, p_ref, o_ref, acc):
        step = pl.program_id(0)

        @pl.when(step == 0)
        def _():
            acc[...] = jnp.zeros_like(acc)

        for i in range(g):
            k = step * g + i

            @pl.when(v_ref[k] > 0)
            def _():
                acc[i_ref[k]] += jnp.sum(p_ref[:, i].astype(F32), axis=0)

        @pl.when(step == slots // g - 1)
        def _():
            o_ref[...] = acc[...].astype(o_ref.dtype)

    return slot_call(
        body, (ids, valid), (parts,),
        [pl.BlockSpec((w_count, g, toks, block), lambda k, i, v: (0, k, 0, 0))],
        jax.ShapeDtypeStruct((blocks_total, toks, block), BF16),
        pl.BlockSpec((blocks_total, toks, block), lambda k, i, v: (0, 0, 0)),
        [pltpu.VMEM((blocks_total, toks, block), F32)], w_count * slots * toks * block, "combine",
        slots // g,
    )


def decoder_grads(ids, tgt, valid, rep, lat, lat_twin, err, err_twin, slots):
    layers, toks, width = err.shape
    blocks, _, half = lat_twin.shape
    g = group_of(slots)

    def body(i_ref, t_ref, v_ref, r_ref, l_ref, lt_ref, e_ref, et_ref, o_ref):
        over = (((0,), (0,)), ((), ()))
        for i in range(g):
            k = pl.program_id(0) * g + i

            @pl.when(v_ref[k] > 0)
            def _():
                t, b = t_ref[k], i_ref[k]
                o_ref[i] = lax.dot_general(
                    l_ref[b], e_ref[t], over, preferred_element_type=F32
                ) + lax.dot_general(lt_ref[b], et_ref[t], over, preferred_element_type=F32)

            @pl.when(v_ref[k] == 0)
            def _():
                o_ref[i] = jnp.zeros_like(o_ref[i])

    return slot_call(
        body, (ids, tgt, valid, rep), (lat, lat_twin, err, err_twin),
        [pl.BlockSpec((blocks, toks, half), lambda k, i, t, v, r: (0, 0, r[0])),
         pl.BlockSpec((blocks, toks, half), lambda k, i, t, v, r: (0, 0, 0)),
         pl.BlockSpec((layers, toks, width), lambda k, i, t, v, r: (0, 0, 0)),
         pl.BlockSpec((layers, toks, width), lambda k, i, t, v, r: (0, 0, 0))],
        jax.ShapeDtypeStruct((slots, half, width), F32),
        pl.BlockSpec((g, half, width), lambda k, i, t, v, r: (k, 0, 0)),
        [], 4 * slots * toks * half * width, "decoder_grads", slots // g,
    )


def local(acts, targets, enc_weight, enc_bias, gate_mask, dec_list, dec_weight):
    layers, tok_rows, width_part = acts.shape
    lat_dev = enc_weight.shape[1]
    slots, block, _ = dec_weight.shape
    per_dev = lat_dev // block
    n, w_count, r_count = lax.axis_size("lay"), lax.axis_size("wid"), lax.axis_size("rep")
    lay, wid, rep = lax.axis_index("lay"), lax.axis_index("wid"), lax.axis_index("rep")
    lat_total = lat_dev * n
    blocks_total = lat_total // block
    latents_layer = lat_total // layers
    blocks_layer = latents_layer // block
    toks = tok_rows // w_count
    rows = tok_rows // n

    tgt = dec_list[:, 1]
    valid = (tgt >= 0).astype(jnp.int32)
    ids = jnp.maximum(dec_list[:, 0] * blocks_layer + dec_list[:, 2], 0)
    tgt = jnp.maximum(tgt, 0)

    here = lax.dynamic_index_in_dim(acts, lay * lat_dev // latents_layer, 0, keepdims=False)
    partial = jnp.dot(here, enc_weight, preferred_element_type=F32).astype(BF16)
    parts = exchange(
        "wid", partial.reshape(w_count, toks, lat_dev), (w_count, toks, lat_dev), (toks, lat_dev),
        lambda x, j: x.at[j], lambda o, j: o.at[j], 0,
    )
    shifted = jnp.sum(parts.astype(F32), axis=0) + enc_bias[None, :]
    shifted = shifted.reshape(toks, per_dev, block).transpose(1, 0, 2)
    keep = lax.dynamic_slice_in_dim(gate_mask, wid * toks, toks, 0).astype(F32).T[:, :, None]
    latent = (smooth_gate(shifted) * keep).astype(BF16)
    lat = gather_latents(latent, 1).reshape(blocks_total, tok_rows, block)

    recon_part = decode(ids, tgt, valid, lat, dec_weight, layers)
    recon_in = exchange(
        "lay", recon_part.reshape(layers, n, rows, width_part), (n, layers, rows, width_part),
        (layers, rows, width_part), lambda x, j: x.at[:, j], lambda o, j: o.at[j], 2,
    )
    recon = jnp.sum(recon_in.astype(F32), axis=0)
    own_target = lax.dynamic_slice_in_dim(targets, lay * rows, rows, 1)
    scale = float(tok_rows * r_count) ** (-0.5)
    own_err = ((recon - own_target.astype(F32)) * scale).astype(BF16)
    err = gather_errors(own_err, 3).reshape(layers, tok_rows, width_part)

    slot_err = slot_errors(tgt, err, dec_weight).reshape(slots, w_count, toks, block)
    slot_in, lat_twin, err_twin, acts_all = slots_and_twin(slot_err, lat, err, here, 4)
    outgoing = combine(ids, valid, slot_in, blocks_total)
    incoming = exchange(
        "lay", outgoing.reshape(n, per_dev, toks, block), (n, per_dev, toks, block),
        (per_dev, toks, block), lambda x, j: x.at[j], lambda o, j: o.at[j], 5,
    )
    dec_out = decoder_grads(
        ids, tgt, valid, rep.reshape(1).astype(jnp.int32), lat, lat_twin, err, err_twin, slots
    )
    latent_error = jnp.sum(incoming.astype(F32), axis=0)
    pre_grad = (latent_error * keep * gate_slope(shifted)).astype(BF16)
    columns = lat_dev // r_count
    pre_grad = pre_grad.transpose(1, 0, 2).reshape(toks, r_count, columns).transpose(1, 0, 2)
    pre_all = gather_pre_grad(pre_grad, 6).reshape(r_count, tok_rows, columns)

    enc_out = lax.dot_general(
        acts_all.reshape(r_count * tok_rows, width_part),
        pre_all.reshape(r_count * tok_rows, columns), (((0,), (0,)), ((), ())),
        preferred_element_type=F32,
    )
    bias_out = jnp.sum(pre_all.astype(F32), axis=(0, 1))
    return (enc_out, bias_out, dec_out)


def solution(mesh):
    return jax.shard_map(
        local,
        mesh=mesh,
        in_specs=(
            P(None, ("grp", "rep"), "wid"),
            P(None, ("grp", "rep"), "wid"),
            P("wid", "lay"),
            P("lay"),
            P(("grp", "rep"), "lay"),
            P("lay", None),
            P("lay", None, "wid"),
        ),
        out_specs=(
            P(("grp", "wid"), ("lay", "rep")),
            P(("grp", "lay", "rep")),
            P(("grp", "lay"), "rep", "wid"),
        ),
        check_vma=False,
    )
```

time: 383 us -> 315 us (0.82)
  Pallas kernels: 342 us -> 282 us
  local copies, waits for them, and re-layouts: 14.1 us -> 5.93 us
    pallas_call x7, Pallas kernels: 291 us -> 240 us  [comm(): pl.pallas_call(body, out_shape=tuple(outs), in_specs=[ANY] * len(args), o...]
    pallas_call x4, Pallas kernels: 51.6 us -> 41.6 us  [slot_call(): pl.pallas_call(body, out_shape=out_shape, grid_spec=pltpu.PrefetchScalarG...]
    unnamed x24 -> x4, local copies, waits for them, and re-layouts: 9.14 us -> 0.01 us
where the time goes in v2:
time: 315 us; the launch traced here: 313 us
  Pallas kernels  282 us (90%)
  other arithmetic  15.6 us (5%)
  matrix products  9.13 us (3%)
  local copies, waits for them, and re-layouts  5.93 us (2%)
    pallas_call x7, Pallas kernels, comm(): pl.pallas_call(body, out_shape=tuple(outs), in_specs=[ANY] * len(args), o...  240 us
    pallas_call x4, Pallas kernels, slot_call(): pl.pallas_call(body, out_shape=out_shape, grid_spec=pltpu.PrefetchScalarG...  41.6 us

profile of v2, /device:TPU:15, one launch (start us, length us, event | category | flops | bytes accessed | tf_op | source)
XLA Modules:
  0.0 313.3 jit_solution(4098461755674247936)
XLA Ops:
  0.7 1.3 fusion.13.v_ref
  1.9 1.3 maximum_bitcast_fusion
  5.3 1.1 dynamic-slice_bitcast_fusion.a_ref
  6.4 4.6 %convolution_convert_fusion = bf16[256,2048]{1,0:T(8,128)(2,1)} fusion(bf16[256,1024]{1,0:T(8,128)(2,1)S(1)} %dynamic-slice_bitcast_fusion.a_ref, bf16[1024,2048]{1,0:T(8,128)(2,1)} %param.9), kind=kOutput, calls=%fused_computation.2 | convolution fusion | flops 1074266112 | bytes 5767168 | tf_op jit(solution)/shard_map/dot_general | solution.py:459
  11.0 13.2 %exchange_0.1 = bf16[2,128,2048]{2,1,0:T(8,128)(2,1)} custom-call(bf16[2,128,2048]{2,1,0:T(8,128)(2,1)} %bitcast.49), custom_call_target="tpu_custom_call" | custom-call | tf_op jit(solution)/shard_map/exchange_0/pallas_call | solution.py:107
  24.2 1.5 convert_reduce_fusion.3
  25.7 1.3 copy.13
  27.0 1.6 copy.14
  28.6 1.2 fusion.5.h_ref
  29.8 47.5 %exchange_1.1 = bf16[32,2,128,256]{3,2,1,0:T(8,128)(2,1)} custom-call(bf16[8,128,256]{2,1,0:T(8,128)(2,1)} %fusion.5.h_ref), custom_call_target="tpu_custom_call" | custom-call | tf_op jit(solution)/shard_map/exchange_1/pallas_call | solution.py:107
  77.3 13.0 %decode.1 = bf16[4,256,1024]{2,1,0:T(8,128)(2,1)} custom-call(s32[21]{0:T(128)} %get-tuple-element.11.i_ref, s32[21]{0:T(128)} %get-tuple-element.12.t_ref, s32[21]{0:T(128)} %fusion.13.v_ref, bf16[32,256,256]{2,1,0:T(8,128)(2,1)} %bitcast.35, bf16[21,256,1024]{2,1,0:T(8,128)(2,1)} %w_ref.3), custom_call_target="tpu_custom_call" | custom-call | flops 2818572288 | bytes 17301504 | tf_op jit(solution)/shard_map/decode/pallas_call | solution.py:302
  90.3 47.1 %exchange_2.1 = bf16[4,4,64,1024]{3,2,1,0:T(8,128)(2,1)} custom-call(bf16[4,4,64,1024]{3,2,1,0:T(8,128)(2,1)} %bitcast.44), custom_call_target="tpu_custom_call" | custom-call | tf_op jit(solution)/shard_map/exchange_2/pallas_call | solution.py:107
  137.4 2.1 convert_reduce_fusion.1
  139.5 2.0 multiply_convert_fusion.e_ref
  141.5 33.1 %exchange_3.1 = bf16[4,4,64,1024]{3,2,1,0:T(8,128)(2,1)} custom-call(bf16[4,64,1024]{2,1,0:T(8,128)(2,1)} %multiply_convert_fusion.e_ref), custom_call_target="tpu_custom_call" | custom-call | tf_op jit(solution)/shard_map/exchange_3/pallas_call | solution.py:107
  174.6 10.7 %slot_errors.1 = bf16[21,256,256]{2,1,0:T(8,128)(2,1)} custom-call(s32[21]{0:T(128)} %get-tuple-element.12.t_ref, bf16[4,256,1024]{2,1,0:T(8,128)(2,1)} %bitcast.38, bf16[21,256,1024]{2,1,0:T(8,128)(2,1)} %w_ref.3), custom_call_target="tpu_custom_call" | custom-call | flops 2818572288 | bytes 15859712 | tf_op jit(solution)/shard_map/slot_errors/pallas_call | solution.py:302
  185.3 35.1 %exchange_4.1 = (bf16[2,21,128,256]{3,2,1,0:T(8,128)(2,1)}, bf16[32,256,128]{2,1,0:T(8,128)(2,1)}, bf16[4,256,1024]{2,1,0:T(8,128)(2,1)}, bf16[2,256,1024]{2,1,0:T(8,128)(2,1)}) custom-call(bf16[21,2,128,256]{3,2,1,0:T(8,128)(2,1)} %bitcast.41, bf16[32,256,256]{2,1,0:T(8,128)(2,1)} %bitcast.36, bf16[4,256,1024]{2,1,0:T(8,128)(2,1)} %bitcast.39, ...), custom_call_target="tpu_custom_call" | custom-call | tf_op jit(solution)/shard_map/exchange_4/pallas_call | solution.py:107
  220.4 5.2 %combine.1 = bf16[32,128,256]{2,1,0:T(8,128)(2,1)} custom-call(s32[21]{0:T(128)} %get-tuple-element.11.i_ref, s32[21]{0:T(128)} %fusion.13.v_ref, bf16[2,21,128,256]{3,2,1,0:T(8,128)(2,1)} %get-tuple-element.8.p_ref), custom_call_target="tpu_custom_call" | custom-call | flops 1376256 | bytes 4849664 | tf_op jit(solution)/shard_map/combine/pallas_call | solution.py:302
  225.6 49.0 %exchange_5.1 = bf16[4,8,128,256]{3,2,1,0:T(8,128)(2,1)} custom-call(bf16[4,8,128,256]{3,2,1,0:T(8,128)(2,1)} %bitcast.43), custom_call_target="tpu_custom_call" | custom-call | tf_op jit(solution)/shard_map/exchange_5/pallas_call | solution.py:107
  274.6 2.0 convert_reduce_fusion
  278.7 12.8 %decoder_grads.1 = f32[21,128,1024]{2,1,0:T(8,128)} custom-call(s32[21]{0:T(128)} %get-tuple-element.11.i_ref, s32[21]{0:T(128)} %get-tuple-element.12.t_ref, s32[21]{0:T(128)} %fusion.13.v_ref, s32[1]{0:T(128)} %bitcast.18.r_ref, bf16[32,256,256]{2,1,0:T(8,128)(2,1)} %bitcast.37, bf16[32,256,128]{2,1,0:T(8,128)(2,1)} %get-tuple-element.9.lt_ref, ...), custom_call_target="tpu_custom_call" | custom-call | flops 2818572288 | bytes 21495808 | tf_op jit(solution)/shard_map/decoder_grads/pallas_call | solution.py:302
  291.5 15.3 %exchange_6.1 = bf16[2,2,128,1024]{3,2,1,0:T(8,128)(2,1)} custom-call(bf16[2,128,1024]{2,1,0:T(8,128)(2,1)} %bitcast.46), custom_call_target="tpu_custom_call" | custom-call | tf_op jit(solution)/shard_map/exchange_6/pallas_call | solution.py:107
  306.8 2.0 convert_reduce_fusion.2
  308.8 4.5 %fusion.14 = f32[1024,1024]{1,0:T(8,128)} fusion(bf16[512,1024]{1,0:T(8,128)(2,1)S(1)} %bitcast.48, bf16[512,1024]{1,0:T(8,128)(2,1)} %bitcast.42), kind=kOutput, calls=%fused_computation.30 | convolution fusion | flops 1073741824 | bytes 6291456 | tf_op jit(solution)/shard_map/dot_general | solution.py:497
  (10 shorter events, 4.1 us)
Async XLA Ops:
  6.4 4.6 %copy-start = (bf16[256,1024]{1,0:T(8,128)(2,1)}, bf16[256,1024]{1,0:T(8,128)(2,1)S(1)}, u32[]{:S(2)}) copy-start(bf16[256,1024]{1,0:T(8,128)(2,1)S(1)} %dynamic-slice_bitcast_fusion.a_ref) | copy-start | bytes 1572868
  291.5 17.3 %copy-start.1 = (bf16[2,256,1024]{2,1,0:T(8,128)(2,1)S(1)}, bf16[2,256,1024]{2,1,0:T(8,128)(2,1)}, u32[]{:S(2)}) copy-start(bf16[2,256,1024]{2,1,0:T(8,128)(2,1)} %get-tuple-element.7) | copy-start | bytes 3145732

commit v3 on v2

--- a/solution.py
+++ b/solution.py
@@ -481,14 +481,15 @@
     slot_err = slot_errors(tgt, err, dec_weight).reshape(slots, w_count, toks, block)
     slot_in, lat_twin, err_twin, acts_all = slots_and_twin(slot_err, lat, err, here, 4)
     outgoing = combine(ids, valid, slot_in, blocks_total)
-    incoming = exchange(
-        "lay", outgoing.reshape(n, per_dev, toks, block), (n, per_dev, toks, block),
-        (per_dev, toks, block), lambda x, j: x.at[j], lambda o, j: o.at[j], 5,
-    )
+    outgoing = outgoing.reshape(n, per_dev, toks, block)
+    incoming = [lax.dynamic_index_in_dim(outgoing, lay, 0, keepdims=False)]
+    for d in range(1, n):
+        part = lax.dynamic_index_in_dim(outgoing, lax.rem(lay + d, n), 0, keepdims=False)
+        incoming.append(lax.ppermute(part, "lay", [(i, (i + d) % n) for i in range(n)]))
     dec_out = decoder_grads(
         ids, tgt, valid, rep.reshape(1).astype(jnp.int32), lat, lat_twin, err, err_twin, slots
     )
-    latent_error = jnp.sum(incoming.astype(F32), axis=0)
+    latent_error = sum(part.astype(F32) for part in incoming)
     pre_grad = (latent_error * keep * gate_slope(shifted)).astype(BF16)
     columns = lat_dev // r_count
     pre_grad = pre_grad.transpose(1, 0, 2).reshape(toks, r_count, columns).transpose(1, 0, 2)

time: 315 us -> 302 us (0.959)
  Pallas kernels: 282 us -> 233 us
  waiting for transfers between devices: 0 us -> 30.2 us
  starting transfers between devices: 0 us -> 4.26 us
    pallas_call x7 -> x6, Pallas kernels: 240 us -> 191 us  [comm(): pl.pallas_call(body, out_shape=tuple(outs), in_specs=[ANY] * len(args), o...]
    ppermute x0 -> x3, waiting for transfers between devices: none -> 30.2 us  [local(): lax.ppermute(part, 'lay', [(i, (i + d) % n) for i in range(n)])]
    ppermute x0 -> x3, starting transfers between devices: none -> 4.26 us  [local(): lax.ppermute(part, 'lay', [(i, (i + d) % n) for i in range(n)])]
  transfers between devices with their start and end apart: 0 -> 3, of which waited for: 0 -> 2; matrix products, arithmetic and copies ran while one was open for 0% -> 0% of each run, Pallas kernels for 0% -> 4%
where the time goes in v3:
time: 302 us; the launch traced here: 299 us
  Pallas kernels  233 us (77%)
  waiting for transfers between devices  30.2 us (10%)
  other arithmetic  13.8 us (5%)
  matrix products  9.13 us (3%)
  local copies, waits for them, and re-layouts  7.79 us (3%)
  starting transfers between devices  4.26 us (1%)
    pallas_call x6, Pallas kernels, comm(): pl.pallas_call(body, out_shape=tuple(outs), in_specs=[ANY] * len(args), o...  191 us
    pallas_call x4, Pallas kernels, slot_call(): pl.pallas_call(body, out_shape=out_shape, grid_spec=pltpu.PrefetchScalarG...  41.9 us
    ppermute x3, waiting for transfers between devices, local(): lax.ppermute(part, 'lay', [(i, (i + d) % n) for i in range(n)])  30.2 us
  transfers between devices with their start and end apart: 3, of which 2 were waited for; matrix products, arithmetic and copies ran while one was open for 0% of the time, Pallas kernels for 4%

profile of v3, /device:TPU:15, one launch (start us, length us, event | category | flops | bytes accessed | tf_op | source)
XLA Modules:
  0.0 298.8 jit_solution(18126379484798321967)
XLA Ops:
  0.6 1.4 maximum_bitcast_fusion
  4.4 4.6 %convolution_convert_fusion = bf16[256,2048]{1,0:T(8,128)(2,1)} fusion(bf16[256,1024]{1,0:T(8,128)(2,1)S(1)} %dynamic-slice_bitcast_fusion.3.a_ref, bf16[1024,2048]{1,0:T(8,128)(2,1)} %param.9), kind=kOutput, calls=%fused_computation.1 | convolution fusion | flops 1074266112 | bytes 5767168 | tf_op jit(solution)/shard_map/dot_general | solution.py:459
  9.0 13.2 %exchange_0.1 = bf16[2,128,2048]{2,1,0:T(8,128)(2,1)} custom-call(bf16[2,128,2048]{2,1,0:T(8,128)(2,1)} %bitcast.68), custom_call_target="tpu_custom_call" | custom-call | tf_op jit(solution)/shard_map/exchange_0/pallas_call | solution.py:107
  22.2 1.5 convert_reduce_fusion.2
  25.0 1.6 copy.14
  27.8 47.5 %exchange_1.1 = bf16[32,2,128,256]{3,2,1,0:T(8,128)(2,1)} custom-call(bf16[8,128,256]{2,1,0:T(8,128)(2,1)} %multiply_convert_fusion.1.h_ref), custom_call_target="tpu_custom_call" | custom-call | tf_op jit(solution)/shard_map/exchange_1/pallas_call | solution.py:107
  75.3 13.2 %decode.1 = bf16[4,256,1024]{2,1,0:T(8,128)(2,1)} custom-call(s32[21]{0:T(128)} %get-tuple-element.14.i_ref, s32[21]{0:T(128)} %get-tuple-element.15.t_ref, s32[21]{0:T(128)} %fusion.11.v_ref, bf16[32,256,256]{2,1,0:T(8,128)(2,1)} %bitcast.53, bf16[21,256,1024]{2,1,0:T(8,128)(2,1)} %w_ref.3), custom_call_target="tpu_custom_call" | custom-call | flops 2818572288 | bytes 17301504 | tf_op jit(solution)/shard_map/decode/pallas_call | solution.py:302
  88.5 47.1 %exchange_2.1 = bf16[4,4,64,1024]{3,2,1,0:T(8,128)(2,1)} custom-call(bf16[4,4,64,1024]{3,2,1,0:T(8,128)(2,1)} %bitcast.63), custom_call_target="tpu_custom_call" | custom-call | tf_op jit(solution)/shard_map/exchange_2/pallas_call | solution.py:107
  135.6 2.1 convert_reduce_fusion
  137.7 2.0 multiply_convert_fusion.e_ref
  139.7 33.1 %exchange_3.1 = bf16[4,4,64,1024]{3,2,1,0:T(8,128)(2,1)} custom-call(bf16[4,64,1024]{2,1,0:T(8,128)(2,1)} %multiply_convert_fusion.e_ref), custom_call_target="tpu_custom_call" | custom-call | tf_op jit(solution)/shard_map/exchange_3/pallas_call | solution.py:107
  172.8 10.7 %slot_errors.1 = bf16[21,256,256]{2,1,0:T(8,128)(2,1)} custom-call(s32[21]{0:T(128)} %get-tuple-element.15.t_ref, bf16[4,256,1024]{2,1,0:T(8,128)(2,1)} %bitcast.56, bf16[21,256,1024]{2,1,0:T(8,128)(2,1)} %w_ref.3), custom_call_target="tpu_custom_call" | custom-call | flops 2818572288 | bytes 15859712 | tf_op jit(solution)/shard_map/slot_errors/pallas_call | solution.py:302
  183.5 35.1 %exchange_4.1 = (bf16[2,21,128,256]{3,2,1,0:T(8,128)(2,1)}, bf16[32,256,128]{2,1,0:T(8,128)(2,1)}, bf16[4,256,1024]{2,1,0:T(8,128)(2,1)}, bf16[2,256,1024]{2,1,0:T(8,128)(2,1)}) custom-call(bf16[21,2,128,256]{3,2,1,0:T(8,128)(2,1)} %bitcast.59, bf16[32,256,256]{2,1,0:T(8,128)(2,1)} %bitcast.54, bf16[4,256,1024]{2,1,0:T(8,128)(2,1)} %bitcast.57, ...), custom_call_target="tpu_custom_call" | custom-call | tf_op jit(solution)/shard_map/exchange_4/pallas_call | solution.py:107
  218.5 5.2 %combine.1 = bf16[32,128,256]{2,1,0:T(8,128)(2,1)} custom-call(s32[21]{0:T(128)} %get-tuple-element.14.i_ref, s32[21]{0:T(128)} %fusion.11.v_ref, bf16[2,21,128,256]{3,2,1,0:T(8,128)(2,1)} %get-tuple-element.8.p_ref), custom_call_target="tpu_custom_call" | custom-call | flops 1376256 | bytes 4849664 | tf_op jit(solution)/shard_map/combine/pallas_call | solution.py:302
  223.7 2.5 dynamic-slice_bitcast_fusion.2
  226.3 2.2 collective-permute-start.2
  228.5 2.1 collective-permute-start
  230.6 12.8 %decoder_grads.1 = f32[21,128,1024]{2,1,0:T(8,128)} custom-call(s32[21]{0:T(128)} %get-tuple-element.14.i_ref, s32[21]{0:T(128)} %get-tuple-element.15.t_ref, s32[21]{0:T(128)} %fusion.11.v_ref, s32[1]{0:T(128)} %bitcast.22.r_ref, bf16[32,256,256]{2,1,0:T(8,128)(2,1)} %bitcast.55, bf16[32,256,128]{2,1,0:T(8,128)(2,1)} %get-tuple-element.9.lt_ref, ...), custom_call_target="tpu_custom_call" | custom-call | flops 2818572288 | bytes 21495808 | tf_op jit(solution)/shard_map/decoder_grads/pallas_call | solution.py:302
  243.4 19.0 %collective-permute-done.1 = bf16[8,128,256]{2,1,0:T(8,128)(2,1)} collective-permute-done((bf16[8,128,256]{2,1,0:T(8,128)(2,1)}, bf16[8,128,256]{2,1,0:T(8,128)(2,1)}, u32[]{:S(2)}, u32[]{:S(2)}) %collective-permute-start.1) | collective-permute-done | bytes 524320 | tf_op jit(solution)/shard_map/ppermute | solution.py:488
  262.3 11.2 %collective-permute-done = bf16[8,128,256]{2,1,0:T(8,128)(2,1)} collective-permute-done((bf16[8,128,256]{2,1,0:T(8,128)(2,1)}, bf16[8,128,256]{2,1,0:T(8,128)(2,1)}, u32[]{:S(2)}, u32[]{:S(2)}) %collective-permute-start) | collective-permute-done | bytes 524320 | tf_op jit(solution)/shard_map/ppermute | solution.py:488
  273.6 2.3 fusion.10
  277.2 15.0 %exchange_6.1 = bf16[2,2,128,1024]{3,2,1,0:T(8,128)(2,1)} custom-call(bf16[2,128,1024]{2,1,0:T(8,128)(2,1)} %bitcast.65), custom_call_target="tpu_custom_call" | custom-call | tf_op jit(solution)/shard_map/exchange_6/pallas_call | solution.py:107
  292.2 2.0 convert_reduce_fusion.1
  294.3 4.5 %fusion.12 = f32[1024,1024]{1,0:T(8,128)} fusion(bf16[512,1024]{1,0:T(8,128)(2,1)S(1)} %bitcast.67, bf16[512,1024]{1,0:T(8,128)(2,1)} %bitcast.60), kind=kOutput, calls=%fused_computation.30 | convolution fusion | flops 1073741824 | bytes 6291456 | tf_op jit(solution)/shard_map/dot_general | solution.py:498
  (18 shorter events, 6.2 us)
Async XLA Ops:
  4.4 4.6 %copy-start = (bf16[256,1024]{1,0:T(8,128)(2,1)}, bf16[256,1024]{1,0:T(8,128)(2,1)S(1)}, u32[]{:S(2)}) copy-start(bf16[256,1024]{1,0:T(8,128)(2,1)S(1)} %dynamic-slice_bitcast_fusion.3.a_ref) | copy-start | bytes 1572868
  23.7 2.9 copy-start.2
  23.7 2.9 copy-start.3
  226.3 17.1 %collective-permute-start.2 = (bf16[8,128,256]{2,1,0:T(8,128)(2,1)}, bf16[8,128,256]{2,1,0:T(8,128)(2,1)S(1)}, u32[]{:S(2)}, u32[]{:S(2)}) collective-permute-start(bf16[8,128,256]{2,1,0:T(8,128)(2,1)} %get-tuple-element.12), channel_id=1, source_target_pairs={{0,12},{4,0},{8,4},{12,8},{1,13},{5,1},{9,5},{13,9},{2,14},{6,2},{... | collective-permute-start | bytes 1572872 | tf_op jit(solution)/shard_map/ppermute | solution.py:488
  228.5 33.9 %collective-permute-start.1 = (bf16[8,128,256]{2,1,0:T(8,128)(2,1)}, bf16[8,128,256]{2,1,0:T(8,128)(2,1)}, u32[]{:S(2)}, u32[]{:S(2)}) collective-permute-start(bf16[8,128,256]{2,1,0:T(8,128)(2,1)} %get-tuple-element.13), channel_id=1, source_target_pairs={{0,8},{4,12},{8,0},{12,4},{1,9},{5,13},{9,1},{13,5},{2,10},{6,14},... | collective-permute-start | bytes 1572872 | tf_op jit(solution)/shard_map/ppermute | solution.py:488
  228.5 45.1 %collective-permute-start = (bf16[8,128,256]{2,1,0:T(8,128)(2,1)}, bf16[8,128,256]{2,1,0:T(8,128)(2,1)}, u32[]{:S(2)}, u32[]{:S(2)}) collective-permute-start(bf16[8,128,256]{2,1,0:T(8,128)(2,1)} %get-tuple-element.11), channel_id=1, source_target_pairs={{0,4},{4,8},{8,12},{12,0},{1,5},{5,9},{9,13},{13,1},{2,6},{6,10},{... | collective-permute-start | bytes 1572872 | tf_op jit(solution)/shard_map/ppermute | solution.py:488
  276.2 18.1 %copy-start.1 = (bf16[2,256,1024]{2,1,0:T(8,128)(2,1)S(1)}, bf16[2,256,1024]{2,1,0:T(8,128)(2,1)}, u32[]{:S(2)}) copy-start(bf16[2,256,1024]{2,1,0:T(8,128)(2,1)} %get-tuple-element.7) | copy-start | bytes 3145732
